TPU v7x, 32 devices: a whole 2x2x4 slice. The times are simulated.
32 devices in a mesh: face: 8 (over z, core), sub: 4 (over y, x).
Axes of the slice: x: 2, y: 2, z: 4, core: 2. Of those that a mesh axis runs over, the one named last changes fastest.
Arguments:
- mesh_latent: bfloat16 [8192, 512], P(('face', 'sub')), may hold values from -6 to 6
- edge_latent: bfloat16 [65536, 512], P(('face', 'sub')), may hold values from -6 to 6
- grid_features: bfloat16 [8192, 384], P(('face', 'sub')), may hold values from -6 to 6
- senders: int32 [65536], P(('face', 'sub')), may hold values from 0 to 383, as said below
- receivers: int32 [65536], P(('face', 'sub')), may hold values from 0 to 255
- send_lists: int32 [32, 4, 32], P(('face', 'sub')), may hold values from -1 to 255, as said below
- link_sources: int32 [16384], P(('face', 'sub')), may hold values from 0 to 255
- link_targets: int32 [16384], P(('face', 'sub')), may hold values from 0 to 255
- node_area: float32 [8192], P(('face', 'sub')), may hold values from 0.25 to 4.5
- grid_weight: bfloat16 [384, 512], P(None, 'sub'), may hold values from -0.3125 to 0.3125
- encode_weight: bfloat16 [1024, 512], P('sub'), may hold values from -0.1875 to 0.1875
- edge_first: bfloat16 [1, 1536, 512], P(None, 'sub'), may hold values from -0.15625 to 0.15625
- edge_second: bfloat16 [1, 512, 512], P(None, 'sub'), may hold values from -0.25 to 0.25
- node_first: bfloat16 [1, 1024, 512], P(None, 'sub'), may hold values from -0.1875 to 0.1875
- node_second: bfloat16 [1, 512, 512], P(None, 'sub'), may hold values from -0.25 to 0.25
Outputs:
- mesh_result: bfloat16 [8192, 512], P(('face', 'sub'))
- edge_result: bfloat16 [65536, 512], P(('face', 'sub'))
- masses: float32 [1, 512], replicated
Inputs may be any that keep to these rules, and one draw needn't show every extreme that they name: `send_lists`: entries are the sending partition's own node numbers, or -1 for an unused slot; in every list the used slots come first, hold distinct nodes and number 32 // 2 or more; for every list number some partition uses all 32 slots. `senders`: A value below 256 names one of the partition's own nodes; 256 + d * 32 + k names slot k of the list with number d that the partition receives, and that slot is always a used one.
All inputs are finite; a program needn't handle non-finite values.
Results may differ from a plain program's by a relative error of at most 0.008.
Values may be sent and summed in bfloat16 or wider, within the bound.
A program may use at most 64 MiB of HBM per device.

v0:
```python
import jax
import jax.numpy as jnp
from jax import lax
from jax.sharding import PartitionSpec as P


def passed_along(value, axis, steps):
    count = lax.axis_size(axis)
    pairs = [(source, (source + steps) % count) for source in range(count)]
    return lax.ppermute(value, axis, pairs)


def fold_rows(weight, operand):
    return jnp.dot(
        operand,
        lax.all_gather(weight, "sub", axis=0, tiled=True),
        preferred_element_type=jnp.float32,
    )


def edge_rows(weight, operand):
    storage = jnp.zeros((1, weight.shape[1]), jnp.bfloat16)
    total = jnp.dot(
        operand,
        lax.all_gather(weight, "sub", axis=0, tiled=True),
        preferred_element_type=jnp.float32,
    )
    return (total, storage)


def along_face(values, offset):
    return passed_along(values, "face", offset)


def along_sub(values, offset):
    return passed_along(values, "sub", offset)


def per_device(
    mesh_latent,
    edge_latent,
    grid_features,
    senders,
    receivers,
    send_lists,
    link_sources,
    link_targets,
    node_area,
    grid_weight,
    encode_weight,
    edge_first,
    edge_second,
    node_first,
    node_second,
):
    node_rows = mesh_latent.shape[0]
    nodes_all = node_rows * lax.axis_size("face") * lax.axis_size("sub")
    grid_latent = jax.nn.silu(
        jnp.dot(
            grid_features,
            lax.all_gather(grid_weight, "sub", axis=1, tiled=True),
            preferred_element_type=jnp.float32,
        )
    ).astype(jnp.bfloat16)

    def project(weight, operand):
        return fold_rows(weight, operand)

    node_ids = jnp.arange(node_rows, dtype=jnp.int32)
    joined = jnp.concatenate(
        [jnp.take(grid_latent, link_sources, axis=0), jnp.take(mesh_latent, link_targets, axis=0)],
        axis=1,
    )
    messages = jax.nn.silu(project(encode_weight, joined)).astype(jnp.bfloat16)
    target_onehot = (link_targets[:, None] == node_ids[None, :]).astype(jnp.bfloat16)
    arriving = lax.dot_general(
        target_onehot, messages, (((0,), (0,)), ((), ())), preferred_element_type=jnp.float32
    )
    latent = (mesh_latent.astype(jnp.float32) + arriving).astype(jnp.bfloat16)
    halo_lists = send_lists[0]
    list_mask = (halo_lists >= 0)[:, :, None]
    receive_onehot = (receivers[:, None] == node_ids[None, :]).astype(jnp.bfloat16)
    edge_state = edge_latent
    picked = jnp.take(latent, jnp.maximum(halo_lists, 0), axis=0)
    picked = jnp.where(list_mask, picked, jnp.zeros((), jnp.bfloat16))
    lower_face = along_face(picked[0], 1)
    upper_face = along_face(picked[1], -1)
    lower_sub = along_sub(picked[2], 1)
    upper_sub = along_sub(picked[3], -1)
    arrived = jnp.concatenate([lower_face, upper_face, lower_sub, upper_sub], axis=0)
    receiving_rows = jnp.take(latent, receivers, axis=0)
    node_table = jnp.concatenate([latent, arrived], axis=0)
    inputs = jnp.concatenate(
        [edge_state, jnp.take(node_table, senders, axis=0), receiving_rows], axis=1
    )
    before, unused_rows = edge_rows(edge_first[0], inputs)
    hidden = jax.nn.silu(before).astype(jnp.bfloat16)
    edge_state = (edge_state.astype(jnp.float32) + project(edge_second[0], hidden)).astype(
        jnp.bfloat16
    )
    incoming = lax.dot_general(
        receive_onehot, edge_state, (((0,), (0,)), ((), ())), preferred_element_type=jnp.float32
    ).astype(jnp.bfloat16)
    node_hidden = jax.nn.silu(
        project(node_first[0], jnp.concatenate([latent, incoming], axis=1))
    ).astype(jnp.bfloat16)
    latent = (latent.astype(jnp.float32) + project(node_second[0], node_hidden)).astype(
        jnp.bfloat16
    )
    totals = [jnp.dot(node_area, latent.astype(jnp.float32), precision=lax.Precision.HIGHEST)]
    stacked = lax.psum(jnp.stack(totals), ("face", "sub"))
    masses = stacked / nodes_all
    return (latent, edge_state, masses)


def solution(mesh):
    in_specs = (
        P(("face", "sub"), None),
        P(("face", "sub"), None),
        P(("face", "sub"), None),
        P(("face", "sub")),
        P(("face", "sub")),
        P(("face", "sub"), None, None),
        P(("face", "sub")),
        P(("face", "sub")),
        P(("face", "sub")),
        P(None, "sub"),
        P("sub", None),
        P(None, "sub", None),
        P(None, "sub", None),
        P(None, "sub", None),
        P(None, "sub", None),
    )
    out_specs = (P(("face", "sub"), None), P(("face", "sub"), None), P())
    return jax.shard_map(
        per_device, mesh=mesh, in_specs=in_specs, out_specs=out_specs, check_vma=False
    )
```

profile of v0, /device:TPU:0, one launch (start us, length us, event | category | flops | bytes accessed | tf_op | source)
XLA Modules:
  0.0 153.9 jit_solution(15797503033091889898)
XLA Ops:
  7.2 0.0 copy-start
  7.2 0.0 all-gather.8.cloned.1.call-start
  7.2 0.7 all-gather.8.cloned.1.call-update
  7.9 0.0 all-gather.10.cloned.1.call-start
  8.0 0.7 all-gather.10.cloned.1.call-update
  8.7 0.0 all-gather.12.cloned.1.call-start
  8.7 0.7 all-gather.12.cloned.1.call-update
  9.4 0.7 compare_select_fusion.2
  10.1 0.7 compare_and_fusion.2
  10.8 0.7 compare_select_fusion.3
  11.5 0.7 compare_and_fusion.3
  12.2 0.7 broadcast_maximum_fusion
  12.8 0.7 compare_bitcast_fusion.1
  13.5 0.7 fusion.46
  14.2 1.3 compare_and_fusion.1
  15.5 0.7 fusion.47
  16.2 1.3 compare_and_fusion
  17.5 12.5 %all_gather.18 = bf16[384,512]{1,0:T(8,128)(2,1)S(1)} all-gather(bf16[384,128]{1,0:T(8,128)(2,1)} %param.26), channel_id=1, replica_groups=mesh['face'=8,'sub'=4] {'sub'}, dimensions={1}, use_global_device_ids=true | all-gather | bytes 491520 | tf_op jit(solution)/shard_map/all_gather | solution.py:61
  30.1 0.1 reshape.70
  30.1 13.3 %all-gather.1 = bf16[1,512,512]{2,1,0:T(8,128)(2,1)} all-gather(bf16[1,128,512]{2,1,0:T(8,128)(2,1)} %param.29), channel_id=3, replica_groups=mesh['face'=8,'sub'=4] {'sub'}, dimensions={1}, use_global_device_ids=true | all-gather | bytes 655360 | tf_op jit(solution)/shard_map/all_gather | solution.py:16
  43.5 10.7 %all-gather.3 = bf16[1,512,512]{2,1,0:T(8,128)(2,1)S(1)} all-gather(bf16[1,128,512]{2,1,0:T(8,128)(2,1)S(1)} %copy-done.3), channel_id=5, replica_groups=mesh['face'=8,'sub'=4] {'sub'}, dimensions={1}, use_global_device_ids=true | all-gather | bytes 655360 | tf_op jit(solution)/shard_map/all_gather | solution.py:16
  54.2 0.4 multiply_convert_fusion.4
  54.6 0.0 copy-start.1
  54.6 2.0 %gather_fusion.3 = bf16[512,512]{1,0:T(8,128)(2,1)S(1)} fusion(bf16[256,512]{1,0:T(8,128)(2,1)S(1)} %multiply_convert_fusion.4, s32[1024]{0:T(1024)S(1)} %pad_clamp_fusion.2), kind=kCustom, calls=%fused_computation.clone | custom fusion | bytes 1050624 | tf_op jit(solution)/shard_map/jit(_take)/gather | solution.py:71
  56.6 2.0 %gather_fusion.4 = bf16[512,512]{1,0:T(8,128)(2,1)S(1)} fusion(bf16[256,512]{1,0:T(8,128)(2,1)S(1)} %copy-done.1, s32[1024]{0:T(1024)S(1)} %pad_clamp_fusion.1), kind=kCustom, calls=%fused_computation.1.clone | custom fusion | bytes 1050624 | tf_op jit(solution)/shard_map/jit(_take)/gather | solution.py:71
  58.5 0.2 broadcast_select_fusion.2
  58.8 0.0 all-gather.8.cloned.1.call-done
  58.8 0.4 copy-done.6
  59.2 2.3 %constant_dynamic-update-slice_fusion.4 = (bf16[384,512]{1,0:T(8,128)(2,1)S(1)}, bf16[256,512]{1,0:T(8,128)(2,1)S(1)}) fusion(bf16[1024,512]{1,0:T(8,128)(2,1)} %all-gather.8.cloned.1.call-done, bf16[512,512]{1,0:T(8,128)(2,1)S(1)} %get-tuple-element.12, bf16[512,512]{1,0:T(8,128)(2,1)S(1)} %get-tuple-element.13, s32[512]{0:T(512)S(1)} %copy-done.6, ...), kind=kOutput, calls=%fused_computation.55 | convolution fusion | flops 675020800 | bytes 2885632 | tf_op jit(solution)/shard_map/dot_general | solution.py:76
  61.5 0.8 gather_fusion
  62.4 0.1 select_select_fusion
  62.5 0.6 slice_bitcast_fusion
  63.1 3.5 %collective-permute-start.1 = (bf16[32,512]{1,0:T(8,128)(2,1)}, bf16[32,512]{1,0:T(8,128)(2,1)}, u32[]{:S(2)}, u32[]{:S(2)}) collective-permute-start(bf16[32,512]{1,0:T(8,128)(2,1)} %get-tuple-element.6), channel_id=1, source_target_pairs={{0,28},{4,0},{8,4},{12,8},{16,12},{20,16},{24,20},{28,24},{1,29},{... | collective-permute-start | bytes 98312 | tf_op jit(solution)/shard_map/ppermute | solution.py:10
  66.7 0.4 collective-permute-start.2
  67.1 2.5 %collective-permute-start.3 = (bf16[32,512]{1,0:T(8,128)(2,1)}, bf16[32,512]{1,0:T(8,128)(2,1)S(1)}, u32[]{:S(2)}, u32[]{:S(2)}) collective-permute-start(bf16[32,512]{1,0:T(8,128)(2,1)} %get-tuple-element.4), channel_id=1, source_target_pairs={{0,3},{1,0},{2,1},{3,2},{4,7},{5,4},{6,5},{7,6},{8,11},{9,8},{10,9... | collective-permute-start | bytes 98312 | tf_op jit(solution)/shard_map/ppermute | solution.py:10
  69.6 7.5 %gather_fusion.2 = bf16[2048,512]{1,0:T(8,128)(2,1)S(1)} fusion(bf16[256,512]{1,0:T(8,128)(2,1)S(1)} %get-tuple-element.11, s32[2048]{0:T(1024)S(1)} %fusion.47), kind=kCustom, calls=%fused_computation.4 | custom fusion | bytes 4202496 | tf_op jit(solution)/shard_map/jit(_take)/gather | solution.py:91
  77.1 2.2 %broadcast_select_fusion = bf16[2048,512]{1,0:T(8,128)(2,1)} fusion(bf16[2048,512]{1,0:T(8,128)(2,1)S(1)} %gather_fusion.2, pred[2048]{0:T(1024)(128)(4,1)} %compare_and_fusion), kind=kLoop, calls=%fused_computation.14 | loop fusion | flops 1048576 | bytes 4196352 | tf_op jit(solution)/shard_map/jit(_take)/select_n | solution.py:91
  79.4 0.8 constant_dynamic-update-slice_fusion.3
  80.1 0.8 constant_dynamic-update-slice_fusion.2
  80.9 7.5 %gather_fusion.1 = bf16[2048,512]{1,0:T(8,128)(2,1)S(1)} fusion(bf16[384,512]{1,0:T(8,128)(2,1)S(1)} %constant_dynamic-update-slice_fusion, s32[2048]{0:T(1024)S(1)} %fusion.46), kind=kCustom, calls=%fused_computation.3 | custom fusion | bytes 4202496 | tf_op jit(solution)/shard_map/jit(_take)/gather | solution.py:94
  88.5 1.6 %broadcast_select_fusion.1 = bf16[2048,512]{1,0:T(8,128)(2,1)} fusion(bf16[2048,512]{1,0:T(8,128)(2,1)S(1)} %gather_fusion.1, pred[2048]{0:T(1024)(128)(4,1)S(1)} %copy-done.5), kind=kLoop, calls=%fused_computation.15 | loop fusion | flops 1048576 | bytes 4196352 | tf_op jit(solution)/shard_map/jit(_take)/select_n | solution.py:94
  90.0 8.5 %add_convert_fusion = bf16[2048,512]{1,0:T(8,128)(2,1)S(1)} fusion(bf16[2048,512]{1,0:T(8,128)(2,1)} %param.18, bf16[2048,512]{1,0:T(8,128)(2,1)} %broadcast_select_fusion, bf16[2048,512]{1,0:T(8,128)(2,1)} %broadcast_select_fusion.1, bf16[1,1536,512]{2,1,0:T(8,128)(2,1)} %all-gather.10.cloned.1.call-done, bf16[1,512,512]{2,1,0:T(8,128)(2,1)} %all-gather.1), kind=kOutput, calls=%fused_computation.11 | convolution fusion | flops 4322230272 | bytes 10485760 | tf_op jit(solution)/shard_map/dot_general | solution.py:14
  98.6 1.8 %fusion.8 = bf16[256,512]{1,0:T(8,128)(2,1)} fusion(bf16[2048,512]{1,0:T(8,128)(2,1)S(1)} %add_convert_fusion, s32[2048]{0:T(1024)S(1)} %copy-done.4), kind=kOutput, calls=%fused_computation.20 | convolution fusion | flops 537526272 | bytes 2367488 | tf_op jit(solution)/shard_map/dot_general | solution.py:101
  100.4 4.8 %all-gather.12.cloned.1.call-done = bf16[1,1024,512]{2,1,0:T(8,128)(2,1)} async-done(((bf16[1,256,512]{2,1,0:T(8,128)(2,1)}), bf16[1,1024,512]{2,1,0:T(8,128)(2,1)}) %all-gather.12.cloned.1.call-update) | async-done | bytes 1048592 | tf_op jit(solution)/shard_map/all_gather | solution.py:16
  105.3 2.0 %fusion.10 = bf16[256,512]{1,0:T(8,128)(2,1)S(1)} fusion(bf16[1,512,512]{2,1,0:T(8,128)(2,1)S(1)} %all-gather.3, bf16[1,1024,512]{2,1,0:T(8,128)(2,1)} %all-gather.12.cloned.1.call-done, bf16[256,512]{1,0:T(8,128)(2,1)} %fusion.8, bf16[256,512]{1,0:T(8,128)(2,1)S(1)} %get-tuple-element.11), kind=kOutput, calls=%fused_computation.22 | convolution fusion | flops 404750336 | bytes 2359296 | tf_op jit(solution)/shard_map/dot_general | solution.py:14
  107.3 0.2 fusion.59
  107.5 39.2 %psum.7 = f32[1,512]{1,0:T(1,128)S(1)} all-reduce(f32[1,512]{1,0:T(1,128)S(1)} %fusion.59), channel_id=1, replica_groups=mesh['face'=8,'sub'=4] {'face','sub'}, use_global_device_ids=true, to_apply=%region_0.2 | all-reduce | flops 512 | bytes 4096 | tf_op jit(solution)/shard_map/psum | solution.py:111
  146.8 0.6 broadcast_multiply_fusion
  (26 shorter events, 0.1 us)
Async XLA Ops:
  7.2 47.0 %copy-start = (bf16[256,384]{1,0:T(8,128)(2,1)S(1)}, bf16[256,384]{1,0:T(8,128)(2,1)}, u32[]{:S(2)}) copy-start(bf16[256,384]{1,0:T(8,128)(2,1)} %param.19) | copy-start | bytes 589828
  7.2 36.3 %copy-start.3 = (bf16[1,128,512]{2,1,0:T(8,128)(2,1)S(1)}, bf16[1,128,512]{2,1,0:T(8,128)(2,1)}, u32[]{:S(2)}) copy-start(bf16[1,128,512]{2,1,0:T(8,128)(2,1)} %param.31) | copy-start | bytes 393220
  7.2 51.6 %all-gather.8.cloned.1.call-start = ((), (), s32[]{:S(2)}) async-start(), calls=%async_computation | async-start | bytes 1310720 | tf_op jit(solution)/shard_map/all_gather | solution.py:16
  7.9 82.1 %all-gather.10.cloned.1.call-start = ((), (), s32[]{:S(2)}) async-start(), calls=%async_computation.1 | async-start | bytes 1966080 | tf_op jit(solution)/shard_map/all_gather | solution.py:25
  8.7 96.6 %all-gather.12.cloned.1.call-start = ((), (), s32[]{:S(2)}) async-start(), calls=%async_computation.2 | async-start | bytes 1310720 | tf_op jit(solution)/shard_map/all_gather | solution.py:16
  54.6 2.0 %copy-start.1 = (bf16[256,512]{1,0:T(8,128)(2,1)S(1)}, bf16[256,512]{1,0:T(8,128)(2,1)}, u32[]{:S(2)}) copy-start(bf16[256,512]{1,0:T(8,128)(2,1)} %param.17) | copy-start | bytes 786436
  58.5 0.7 copy-start.6
  63.1 16.2 %collective-permute-start = (bf16[32,512]{1,0:T(8,128)(2,1)}, bf16[32,512]{1,0:T(8,128)(2,1)}, u32[]{:S(2)}, u32[]{:S(2)}) collective-permute-start(bf16[32,512]{1,0:T(8,128)(2,1)} %get-tuple-element.7), channel_id=1, source_target_pairs={{0,4},{4,8},{8,12},{12,16},{16,20},{20,24},{24,28},{28,0},{1,5},{5... | collective-permute-start | bytes 98312 | tf_op jit(solution)/shard_map/ppermute | solution.py:10
  63.1 17.0 %collective-permute-start.1 = (bf16[32,512]{1,0:T(8,128)(2,1)}, bf16[32,512]{1,0:T(8,128)(2,1)}, u32[]{:S(2)}, u32[]{:S(2)}) collective-permute-start(bf16[32,512]{1,0:T(8,128)(2,1)} %get-tuple-element.6), channel_id=1, source_target_pairs={{0,28},{4,0},{8,4},{12,8},{16,12},{20,16},{24,20},{28,24},{1,29},{... | collective-permute-start | bytes 98312 | tf_op jit(solution)/shard_map/ppermute | solution.py:10
  66.7 14.2 %collective-permute-start.2 = (bf16[32,512]{1,0:T(8,128)(2,1)}, bf16[32,512]{1,0:T(8,128)(2,1)S(1)}, u32[]{:S(2)}, u32[]{:S(2)}) collective-permute-start(bf16[32,512]{1,0:T(8,128)(2,1)} %get-tuple-element.5), channel_id=1, source_target_pairs={{0,1},{1,2},{2,3},{3,0},{4,5},{5,6},{6,7},{7,4},{8,9},{9,10},{10,1... | collective-permute-start | bytes 98312 | tf_op jit(solution)/shard_map/ppermute | solution.py:10
  67.1 13.8 %collective-permute-start.3 = (bf16[32,512]{1,0:T(8,128)(2,1)}, bf16[32,512]{1,0:T(8,128)(2,1)S(1)}, u32[]{:S(2)}, u32[]{:S(2)}) collective-permute-start(bf16[32,512]{1,0:T(8,128)(2,1)} %get-tuple-element.4), channel_id=1, source_target_pairs={{0,3},{1,0},{2,1},{3,2},{4,7},{5,4},{6,5},{7,6},{8,11},{9,8},{10,9... | collective-permute-start | bytes 98312 | tf_op jit(solution)/shard_map/ppermute | solution.py:10
  80.9 7.6 %copy-start.5 = (pred[2048]{0:T(1024)(128)(4,1)S(1)}, pred[2048]{0:T(1024)(128)(4,1)}, u32[]{:S(2)}) copy-start(pred[2048]{0:T(1024)(128)(4,1)} %compare_and_fusion.1) | copy-start | bytes 6148
  90.0 8.5 %copy-start.4 = (s32[2048]{0:T(1024)S(1)}, s32[2048]{0:T(1024)}, u32[]{:S(2)}) copy-start(s32[2048]{0:T(1024)} %param.21) | copy-start | bytes 24580
  98.6 8.7 %copy-start.8 = (bf16[2048,512]{1,0:T(8,128)(2,1)}, bf16[2048,512]{1,0:T(8,128)(2,1)S(1)}, u32[]{:S(2)}) copy-start(bf16[2048,512]{1,0:T(8,128)(2,1)S(1)} %add_convert_fusion) | copy-start | bytes 6291460
  100.4 6.9 %copy-start.7 = (f32[256]{0:T(256)S(1)}, f32[256]{0:T(256)}, u32[]{:S(2)}) copy-start(f32[256]{0:T(256)} %param.25) | copy-start | bytes 3076
  107.3 40.1 %copy-start.2 = (bf16[256,512]{1,0:T(8,128)(2,1)}, bf16[256,512]{1,0:T(8,128)(2,1)S(1)}, u32[]{:S(2)}) copy-start(bf16[256,512]{1,0:T(8,128)(2,1)S(1)} %fusion.10) | copy-start | bytes 786436
Sparse Core Ops, SparseCore 0:
  9.8 32.7 all-gather.7
  44.4 32.7 all-gather.9
  79.1 26.1 all-gather.11
where the time goes:
time: 155 us; the launch traced here: 154 us
  blocking collectives  75.8 us (49%)
  local copies, waits for them, and re-layouts  22.6 us (15%)
  matrix products  15.3 us (10%)
  between operations  14 us (9%)
  other arithmetic  12.7 us (8%)
  waiting for transfers between devices  6.92 us (4%)
  starting transfers between devices  6.58 us (4%)
    psum x1, blocking collectives, per_device(): stacked = lax.psum(jnp.stack(totals), ('face', 'sub'))  39.2 us
    all_gather x2, blocking collectives, fold_rows(): lax.all_gather(weight, 'sub', axis=0, tiled=True)  24 us
    all_gather x1, blocking collectives, per_device(): lax.all_gather(grid_weight, 'sub', axis=1, tiled=True)  12.5 us
    dot_general x2, matrix products, fold_rows(): jnp.dot(operand, lax.all_gather(weight, 'sub', axis=0, tiled=True), prefe...  10.5 us
    gather x1, local copies, waits for them, and re-layouts, per_device(): jnp.take(node_table, senders, axis=0)  7.54 us
    gather x1, local copies, waits for them, and re-layouts, per_device(): receiving_rows = jnp.take(latent, receivers, axis=0)  7.53 us
    ppermute x4, starting transfers between devices, passed_along(): return lax.ppermute(value, axis, pairs)  6.47 us
    all_gather x2, waiting for transfers between devices, fold_rows(): lax.all_gather(weight, 'sub', axis=0, tiled=True)  4.85 us
  transfers between devices with their start and end apart: 7, of which 1 were waited for; matrix products, arithmetic and copies ran while one was open for 31% of the time, Pallas kernels for 0%

commit v1 on v0

--- a/solution.py
+++ b/solution.py
@@ -108,7 +108,7 @@
         jnp.bfloat16
     )
     totals = [jnp.dot(node_area, latent.astype(jnp.float32), precision=lax.Precision.HIGHEST)]
-    stacked = lax.psum(jnp.stack(totals), ("face", "sub"))
+    stacked = lax.psum(lax.psum(jnp.stack(totals), "sub"), "face")
     masses = stacked / nodes_all
     return (latent, edge_state, masses)
 

time: 155 us -> 139 us (0.90)
  blocking collectives: 75.8 us -> 59.6 us
    psum x1 -> x2, blocking collectives: 39.2 us -> 23.1 us  [per_device(): stacked = lax.psum(lax.psum(jnp.stack(totals), 'sub'), 'face')]
  transfers between devices with their start and end apart: 7 -> 7, of which waited for: 1 -> 1; matrix products, arithmetic and copies ran while one was open for 31% -> 34% of each run, Pallas kernels for 0% -> 0%
where the time goes in v1:
time: 139 us; the launch traced here: 138 us
  blocking collectives  59.6 us (43%)
  local copies, waits for them, and re-layouts  22.6 us (16%)
  matrix products  15.3 us (11%)
  between operations  14 us (10%)
  other arithmetic  12.8 us (9%)
  waiting for transfers between devices  6.83 us (5%)
  starting transfers between devices  6.58 us (5%)
    all_gather x2, blocking collectives, fold_rows(): lax.all_gather(weight, 'sub', axis=0, tiled=True)  24 us
    psum x2, blocking collectives, per_device(): stacked = lax.psum(lax.psum(jnp.stack(totals), 'sub'), 'face')  23.1 us
    all_gather x1, blocking collectives, per_device(): lax.all_gather(grid_weight, 'sub', axis=1, tiled=True)  12.5 us
    dot_general x2, matrix products, fold_rows(): jnp.dot(operand, lax.all_gather(weight, 'sub', axis=0, tiled=True), prefe...  10.6 us
    gather x1, local copies, waits for them, and re-layouts, per_device(): jnp.take(node_table, senders, axis=0)  7.54 us
    gather x1, local copies, waits for them, and re-layouts, per_device(): receiving_rows = jnp.take(latent, receivers, axis=0)  7.53 us
    ppermute x4, starting transfers between devices, passed_along(): return lax.ppermute(value, axis, pairs)  6.47 us
    all_gather x2, waiting for transfers between devices, fold_rows(): lax.all_gather(weight, 'sub', axis=0, tiled=True)  4.76 us
  transfers between devices with their start and end apart: 7, of which 1 were waited for; matrix products, arithmetic and copies ran while one was open for 34% of the time, Pallas kernels for 0%

profile of v1, /device:TPU:0, one launch (start us, length us, event | category | flops | bytes accessed | tf_op | source)
XLA Modules:
  0.0 137.7 jit_solution(8272117815122790294)
XLA Ops:
  7.2 0.0 copy-start
  7.2 0.0 all-gather.8.cloned.1.call-start
  7.2 0.7 all-gather.8.cloned.1.call-update
  7.9 0.0 all-gather.10.cloned.1.call-start
  8.0 0.7 all-gather.10.cloned.1.call-update
  8.7 0.0 all-gather.12.cloned.1.call-start
  8.7 0.7 all-gather.12.cloned.1.call-update
  9.4 0.7 compare_select_fusion.2
  10.1 0.7 compare_and_fusion.2
  10.8 0.7 compare_select_fusion.3
  11.5 0.7 compare_and_fusion.3
  12.2 0.7 broadcast_maximum_fusion
  12.8 0.7 compare_bitcast_fusion.1
  13.5 0.7 fusion.46
  14.2 1.3 compare_and_fusion.1
  15.5 0.7 fusion.47
  16.2 1.3 compare_and_fusion
  17.5 12.5 %all_gather.18 = bf16[384,512]{1,0:T(8,128)(2,1)S(1)} all-gather(bf16[384,128]{1,0:T(8,128)(2,1)} %param.26), channel_id=1, replica_groups=mesh['face'=8,'sub'=4] {'sub'}, dimensions={1}, use_global_device_ids=true | all-gather | bytes 491520 | tf_op jit(solution)/shard_map/all_gather | solution.py:61
  30.1 0.1 reshape.70
  30.1 13.3 %all-gather.1 = bf16[1,512,512]{2,1,0:T(8,128)(2,1)} all-gather(bf16[1,128,512]{2,1,0:T(8,128)(2,1)} %param.29), channel_id=3, replica_groups=mesh['face'=8,'sub'=4] {'sub'}, dimensions={1}, use_global_device_ids=true | all-gather | bytes 655360 | tf_op jit(solution)/shard_map/all_gather | solution.py:16
  43.5 10.7 %all-gather.3 = bf16[1,512,512]{2,1,0:T(8,128)(2,1)S(1)} all-gather(bf16[1,128,512]{2,1,0:T(8,128)(2,1)S(1)} %copy-done.3), channel_id=5, replica_groups=mesh['face'=8,'sub'=4] {'sub'}, dimensions={1}, use_global_device_ids=true | all-gather | bytes 655360 | tf_op jit(solution)/shard_map/all_gather | solution.py:16
  54.2 0.4 multiply_convert_fusion.4
  54.6 2.0 %gather_fusion.3 = bf16[512,512]{1,0:T(8,128)(2,1)S(1)} fusion(bf16[256,512]{1,0:T(8,128)(2,1)S(1)} %multiply_convert_fusion.4, s32[1024]{0:T(1024)S(1)} %pad_clamp_fusion.2), kind=kCustom, calls=%fused_computation.clone | custom fusion | bytes 1050624 | tf_op jit(solution)/shard_map/jit(_take)/gather | solution.py:71
  56.6 2.0 %gather_fusion.4 = bf16[512,512]{1,0:T(8,128)(2,1)S(1)} fusion(bf16[256,512]{1,0:T(8,128)(2,1)S(1)} %copy-done.1, s32[1024]{0:T(1024)S(1)} %pad_clamp_fusion.1), kind=kCustom, calls=%fused_computation.1.clone | custom fusion | bytes 1050624 | tf_op jit(solution)/shard_map/jit(_take)/gather | solution.py:71
  58.5 0.2 broadcast_select_fusion.2
  58.8 0.0 all-gather.8.cloned.1.call-done
  58.8 0.4 copy-done.6
  59.2 2.3 %constant_dynamic-update-slice_fusion.4 = (bf16[384,512]{1,0:T(8,128)(2,1)S(1)}, bf16[256,512]{1,0:T(8,128)(2,1)S(1)}) fusion(bf16[1024,512]{1,0:T(8,128)(2,1)} %all-gather.8.cloned.1.call-done, bf16[512,512]{1,0:T(8,128)(2,1)S(1)} %get-tuple-element.12, bf16[512,512]{1,0:T(8,128)(2,1)S(1)} %get-tuple-element.13, s32[512]{0:T(512)S(1)} %copy-done.6, ...), kind=kOutput, calls=%fused_computation.55 | convolution fusion | flops 675020800 | bytes 2885632 | tf_op jit(solution)/shard_map/dot_general | solution.py:76
  61.5 0.8 gather_fusion
  62.4 0.1 select_select_fusion
  62.5 0.7 slice_bitcast_fusion
  63.2 3.5 %collective-permute-start.1 = (bf16[32,512]{1,0:T(8,128)(2,1)}, bf16[32,512]{1,0:T(8,128)(2,1)}, u32[]{:S(2)}, u32[]{:S(2)}) collective-permute-start(bf16[32,512]{1,0:T(8,128)(2,1)} %get-tuple-element.6), channel_id=1, source_target_pairs={{0,28},{4,0},{8,4},{12,8},{16,12},{20,16},{24,20},{28,24},{1,29},{... | collective-permute-start | bytes 98312 | tf_op jit(solution)/shard_map/ppermute | solution.py:10
  66.7 0.4 collective-permute-start.2
  67.1 2.5 %collective-permute-start.3 = (bf16[32,512]{1,0:T(8,128)(2,1)}, bf16[32,512]{1,0:T(8,128)(2,1)S(1)}, u32[]{:S(2)}, u32[]{:S(2)}) collective-permute-start(bf16[32,512]{1,0:T(8,128)(2,1)} %get-tuple-element.4), channel_id=1, source_target_pairs={{0,3},{1,0},{2,1},{3,2},{4,7},{5,4},{6,5},{7,6},{8,11},{9,8},{10,9... | collective-permute-start | bytes 98312 | tf_op jit(solution)/shard_map/ppermute | solution.py:10
  69.6 7.5 %gather_fusion.2 = bf16[2048,512]{1,0:T(8,128)(2,1)S(1)} fusion(bf16[256,512]{1,0:T(8,128)(2,1)S(1)} %get-tuple-element.11, s32[2048]{0:T(1024)S(1)} %fusion.47), kind=kCustom, calls=%fused_computation.4 | custom fusion | bytes 4202496 | tf_op jit(solution)/shard_map/jit(_take)/gather | solution.py:91
  77.2 2.2 %broadcast_select_fusion = bf16[2048,512]{1,0:T(8,128)(2,1)} fusion(bf16[2048,512]{1,0:T(8,128)(2,1)S(1)} %gather_fusion.2, pred[2048]{0:T(1024)(128)(4,1)} %compare_and_fusion), kind=kLoop, calls=%fused_computation.14 | loop fusion | flops 1048576 | bytes 4196352 | tf_op jit(solution)/shard_map/jit(_take)/select_n | solution.py:91
  79.4 0.8 constant_dynamic-update-slice_fusion.3
  80.1 0.8 constant_dynamic-update-slice_fusion.2
  81.0 7.5 %gather_fusion.1 = bf16[2048,512]{1,0:T(8,128)(2,1)S(1)} fusion(bf16[384,512]{1,0:T(8,128)(2,1)S(1)} %constant_dynamic-update-slice_fusion, s32[2048]{0:T(1024)S(1)} %fusion.46), kind=kCustom, calls=%fused_computation.3 | custom fusion | bytes 4202496 | tf_op jit(solution)/shard_map/jit(_take)/gather | solution.py:94
  88.5 1.6 %broadcast_select_fusion.1 = bf16[2048,512]{1,0:T(8,128)(2,1)} fusion(bf16[2048,512]{1,0:T(8,128)(2,1)S(1)} %gather_fusion.1, pred[2048]{0:T(1024)(128)(4,1)S(1)} %copy-done.5), kind=kLoop, calls=%fused_computation.15 | loop fusion | flops 1048576 | bytes 4196352 | tf_op jit(solution)/shard_map/jit(_take)/select_n | solution.py:94
  90.1 8.6 %add_convert_fusion = bf16[2048,512]{1,0:T(8,128)(2,1)S(1)} fusion(bf16[2048,512]{1,0:T(8,128)(2,1)} %param.18, bf16[2048,512]{1,0:T(8,128)(2,1)} %broadcast_select_fusion, bf16[2048,512]{1,0:T(8,128)(2,1)} %broadcast_select_fusion.1, bf16[1,1536,512]{2,1,0:T(8,128)(2,1)} %all-gather.10.cloned.1.call-done, bf16[1,512,512]{2,1,0:T(8,128)(2,1)} %all-gather.1), kind=kOutput, calls=%fused_computation.11 | convolution fusion | flops 4322230272 | bytes 10485760 | tf_op jit(solution)/shard_map/dot_general | solution.py:14
  98.7 1.8 %fusion.8 = bf16[256,512]{1,0:T(8,128)(2,1)} fusion(bf16[2048,512]{1,0:T(8,128)(2,1)S(1)} %add_convert_fusion, s32[2048]{0:T(1024)S(1)} %copy-done.4), kind=kOutput, calls=%fused_computation.20 | convolution fusion | flops 537526272 | bytes 2367488 | tf_op jit(solution)/shard_map/dot_general | solution.py:101
  100.5 4.7 %all-gather.12.cloned.1.call-done = bf16[1,1024,512]{2,1,0:T(8,128)(2,1)} async-done(((bf16[1,256,512]{2,1,0:T(8,128)(2,1)}), bf16[1,1024,512]{2,1,0:T(8,128)(2,1)}) %all-gather.12.cloned.1.call-update) | async-done | bytes 1048592 | tf_op jit(solution)/shard_map/all_gather | solution.py:16
  105.2 2.0 %fusion.10 = bf16[256,512]{1,0:T(8,128)(2,1)S(1)} fusion(bf16[1,512,512]{2,1,0:T(8,128)(2,1)S(1)} %all-gather.3, bf16[1,1024,512]{2,1,0:T(8,128)(2,1)} %all-gather.12.cloned.1.call-done, bf16[256,512]{1,0:T(8,128)(2,1)} %fusion.8, bf16[256,512]{1,0:T(8,128)(2,1)S(1)} %get-tuple-element.11), kind=kOutput, calls=%fused_computation.22 | convolution fusion | flops 404750336 | bytes 2359296 | tf_op jit(solution)/shard_map/dot_general | solution.py:14
  107.3 0.2 fusion.59
  107.5 8.9 %psum.14 = f32[1,512]{1,0:T(1,128)S(1)} all-reduce(f32[1,512]{1,0:T(1,128)S(1)} %fusion.59), channel_id=1, replica_groups=mesh['face'=8,'sub'=4] {'sub'}, use_global_device_ids=true, to_apply=%region_0.2 | all-reduce | flops 512 | bytes 4096 | tf_op jit(solution)/shard_map/psum | solution.py:111
  116.4 14.1 %psum.15 = f32[1,512]{1,0:T(1,128)S(1)} all-reduce(f32[1,512]{1,0:T(1,128)S(1)} %psum.14), channel_id=1, replica_groups=mesh['face'=8,'sub'=4] {'face'}, use_global_device_ids=true, to_apply=%region_1.3 | all-reduce | flops 512 | bytes 4096 | tf_op jit(solution)/shard_map/psum | solution.py:111
  130.6 0.6 broadcast_multiply_fusion
  (27 shorter events, 0.1 us)
Async XLA Ops:
  7.2 47.0 %copy-start = (bf16[256,384]{1,0:T(8,128)(2,1)S(1)}, bf16[256,384]{1,0:T(8,128)(2,1)}, u32[]{:S(2)}) copy-start(bf16[256,384]{1,0:T(8,128)(2,1)} %param.19) | copy-start | bytes 589828
  7.2 36.3 %copy-start.3 = (bf16[1,128,512]{2,1,0:T(8,128)(2,1)S(1)}, bf16[1,128,512]{2,1,0:T(8,128)(2,1)}, u32[]{:S(2)}) copy-start(bf16[1,128,512]{2,1,0:T(8,128)(2,1)} %param.31) | copy-start | bytes 393220
  7.2 51.6 %all-gather.8.cloned.1.call-start = ((), (), s32[]{:S(2)}) async-start(), calls=%async_computation | async-start | bytes 1310720 | tf_op jit(solution)/shard_map/all_gather | solution.py:16
  7.9 82.2 %all-gather.10.cloned.1.call-start = ((), (), s32[]{:S(2)}) async-start(), calls=%async_computation.1 | async-start | bytes 1966080 | tf_op jit(solution)/shard_map/all_gather | solution.py:25
  8.7 96.6 %all-gather.12.cloned.1.call-start = ((), (), s32[]{:S(2)}) async-start(), calls=%async_computation.2 | async-start | bytes 1310720 | tf_op jit(solution)/shard_map/all_gather | solution.py:16
  54.6 2.0 %copy-start.1 = (bf16[256,512]{1,0:T(8,128)(2,1)S(1)}, bf16[256,512]{1,0:T(8,128)(2,1)}, u32[]{:S(2)}) copy-start(bf16[256,512]{1,0:T(8,128)(2,1)} %param.17) | copy-start | bytes 786436
  58.5 0.7 copy-start.6
  63.2 16.2 %collective-permute-start = (bf16[32,512]{1,0:T(8,128)(2,1)}, bf16[32,512]{1,0:T(8,128)(2,1)}, u32[]{:S(2)}, u32[]{:S(2)}) collective-permute-start(bf16[32,512]{1,0:T(8,128)(2,1)} %get-tuple-element.7), channel_id=1, source_target_pairs={{0,4},{4,8},{8,12},{12,16},{16,20},{20,24},{24,28},{28,0},{1,5},{5... | collective-permute-start | bytes 98312 | tf_op jit(solution)/shard_map/ppermute | solution.py:10
  63.2 17.0 %collective-permute-start.1 = (bf16[32,512]{1,0:T(8,128)(2,1)}, bf16[32,512]{1,0:T(8,128)(2,1)}, u32[]{:S(2)}, u32[]{:S(2)}) collective-permute-start(bf16[32,512]{1,0:T(8,128)(2,1)} %get-tuple-element.6), channel_id=1, source_target_pairs={{0,28},{4,0},{8,4},{12,8},{16,12},{20,16},{24,20},{28,24},{1,29},{... | collective-permute-start | bytes 98312 | tf_op jit(solution)/shard_map/ppermute | solution.py:10
  66.7 14.2 %collective-permute-start.2 = (bf16[32,512]{1,0:T(8,128)(2,1)}, bf16[32,512]{1,0:T(8,128)(2,1)S(1)}, u32[]{:S(2)}, u32[]{:S(2)}) collective-permute-start(bf16[32,512]{1,0:T(8,128)(2,1)} %get-tuple-element.5), channel_id=1, source_target_pairs={{0,1},{1,2},{2,3},{3,0},{4,5},{5,6},{6,7},{7,4},{8,9},{9,10},{10,1... | collective-permute-start | bytes 98312 | tf_op jit(solution)/shard_map/ppermute | solution.py:10
  67.1 13.8 %collective-permute-start.3 = (bf16[32,512]{1,0:T(8,128)(2,1)}, bf16[32,512]{1,0:T(8,128)(2,1)S(1)}, u32[]{:S(2)}, u32[]{:S(2)}) collective-permute-start(bf16[32,512]{1,0:T(8,128)(2,1)} %get-tuple-element.4), channel_id=1, source_target_pairs={{0,3},{1,0},{2,1},{3,2},{4,7},{5,4},{6,5},{7,6},{8,11},{9,8},{10,9... | collective-permute-start | bytes 98312 | tf_op jit(solution)/shard_map/ppermute | solution.py:10
  80.9 7.6 %copy-start.5 = (pred[2048]{0:T(1024)(128)(4,1)S(1)}, pred[2048]{0:T(1024)(128)(4,1)}, u32[]{:S(2)}) copy-start(pred[2048]{0:T(1024)(128)(4,1)} %compare_and_fusion.1) | copy-start | bytes 6148
  90.1 8.6 %copy-start.4 = (s32[2048]{0:T(1024)S(1)}, s32[2048]{0:T(1024)}, u32[]{:S(2)}) copy-start(s32[2048]{0:T(1024)} %param.21) | copy-start | bytes 24580
  98.7 8.6 %copy-start.8 = (bf16[2048,512]{1,0:T(8,128)(2,1)}, bf16[2048,512]{1,0:T(8,128)(2,1)S(1)}, u32[]{:S(2)}) copy-start(bf16[2048,512]{1,0:T(8,128)(2,1)S(1)} %add_convert_fusion) | copy-start | bytes 6291460
  100.5 6.8 %copy-start.7 = (f32[256]{0:T(256)S(1)}, f32[256]{0:T(256)}, u32[]{:S(2)}) copy-start(f32[256]{0:T(256)} %param.25) | copy-start | bytes 3076
  107.3 23.9 %copy-start.2 = (bf16[256,512]{1,0:T(8,128)(2,1)}, bf16[256,512]{1,0:T(8,128)(2,1)S(1)}, u32[]{:S(2)}) copy-start(bf16[256,512]{1,0:T(8,128)(2,1)S(1)} %fusion.10) | copy-start | bytes 786436
Sparse Core Ops, SparseCore 0:
  9.8 32.6 all-gather.7
  44.4 32.7 all-gather.9
  79.0 26.1 all-gather.11
